TPU v7x, 512 devices: a whole 4x4x16 slice. The times are simulated.
512 devices in a mesh: seq: 64 (over x, z), head: 8 (over y, core).
Axes of the slice: x: 4, y: 4, z: 16, core: 2. Of those that a mesh axis runs over, the one named last changes fastest.
Arguments:
- queries: bfloat16 [8192, 32, 128], P('seq', 'head'), may hold values from -6 to 6
- key_vectors: bfloat16 [8192, 32, 128], P('seq', 'head'), may hold values from -6 to 6
- values: bfloat16 [8192, 32, 128], P('seq', 'head'), may hold values from -6 to 6
- out_grad: bfloat16 [8192, 32, 128], P('seq', 'head'), may hold values from -6 to 6
- hidden_in: bfloat16 [8192, 2048], P('seq'), may hold values from -6 to 6
- decay_weight: bfloat16 [2048, 32], P(None, 'head'), may hold values from -0.125 to 0.125
- write_weight: bfloat16 [2048, 32], P(None, 'head'), may hold values from -0.125 to 0.125
- decay_bias: float32 [32], P('head'), may hold values from -2 to 2
- decay_log: float32 [32], P('head'), may hold values from -11 to -2
- write_bias: float32 [32], P('head'), may hold values from -9 to 0
- start_state: float32 [64, 32, 128, 128], P('seq', 'head'), may hold values from -4 to 4
Outputs:
- grad_queries: bfloat16 [8192, 32, 128], P('seq', 'head')
- grad_keys: bfloat16 [8192, 32, 128], P('seq', 'head')
- grad_values: bfloat16 [8192, 32, 128], P('seq', 'head')
- grad_hidden: bfloat16 [8192, 2048], P('seq', 'head')
- grad_decay_weight: float32 [2048, 32], P(None, 'head')
- grad_write_weight: float32 [2048, 32], P(None, 'head')
All inputs are finite; a program needn't handle non-finite values.
Results may differ from a plain program's by a relative error of at most 0.014.
Values may be sent and summed in bfloat16 or wider, within the bound.
A program may use at most 64 MiB of HBM per device.

v0:
```python
from functools import partial

import jax
import jax.numpy as jnp
from jax import lax
from jax.sharding import Mesh
from jax.sharding import PartitionSpec as P

SEQ = ("seq_0", "seq_1")


EPSILON = 1e-06
PRECISION_MAXIMUM = lax.Precision.HIGHEST


def nothing_yet(array, identity):
    return jax.tree.map(
        lambda part, zero: jnp.zeros_like(part) + jnp.asarray(zero, part.dtype), array, identity
    )


def carried_in(array, axes, combine, identity):
    before = start = nothing_yet(array, identity)
    so_far = array
    for axis in reversed(axes):
        count, place = (lax.axis_size(axis), lax.axis_index(axis))
        pieces = jax.tree.map(lambda part: lax.all_gather(part, axis), so_far)
        inside, so_far = (start, start)
        for k in reversed(range(count)):
            passed = k > place
            so_far = combine(so_far, jax.tree.map(lambda part: part[k], pieces))
            inside = jax.tree.map(lambda new, old: jnp.where(passed, new, old), so_far, inside)
        before = combine(inside, before)
    return before


def sent_to_all(array, axis):
    count = lax.axis_size(axis)
    return lax.all_to_all(
        jnp.broadcast_to(array[None], (count, *array.shape)), axis, 0, 0, tiled=True
    )


def over_copies(array, axis):
    everything = sent_to_all(array, axis)
    return jnp.sum(everything.astype(jnp.float32), axis=0)


def rows_first(arrays, axis, dims):
    turned = [jnp.moveaxis(a, dim, 0) for a, dim in zip(arrays, dims)]
    both = jnp.concatenate([t.reshape(len(t), -1) for t in turned], axis=1)
    out, at, outs = (lax.all_gather(both, axis, axis=0, tiled=True), 0, [])
    for t, dim in zip(turned, dims):
        slab = out[:, at : at + t[0].size].reshape(-1, *t.shape[1:])
        outs.append(jnp.moveaxis(slab, 0, dim))
        at += t[0].size
    return tuple(outs)


def block_forward(
    decay_log,
    decay_bias,
    write_bias,
    queries,
    key_vectors,
    values,
    decay_logit,
    write_logit,
    initial_state,
):
    normalized_queries = queries * lax.rsqrt(
        jnp.sum(queries * queries, axis=-1, keepdims=True) + EPSILON
    )
    normalized_keys = key_vectors * lax.rsqrt(
        jnp.sum(key_vectors * key_vectors, axis=-1, keepdims=True) + EPSILON
    )
    write_rate = jax.nn.sigmoid(write_logit + write_bias)
    log_decay = -jnp.exp(decay_log) * jax.nn.softplus(decay_logit + decay_bias)
    log_prefix = jnp.cumsum(log_decay, axis=0).T
    block_size = queries.shape[0]
    positions = jnp.arange(block_size, dtype=jnp.int32)
    lower_mask = positions[:, None] >= positions[None, :]
    strict_mask = positions[:, None] > positions[None, :]
    log_gaps = jnp.where(lower_mask, log_prefix[:, :, None] - log_prefix[:, None, :], 0.0)
    decay_ratio = jnp.where(lower_mask, jnp.exp(log_gaps), 0.0)
    key_gram = jnp.einsum(
        "ihk,jhk->hij", normalized_keys, normalized_keys, precision=PRECISION_MAXIMUM
    )
    coupling = jnp.where(strict_mask, write_rate.T[:, :, None] * decay_ratio * key_gram, 0.0)
    unit_lower = coupling + jnp.eye(block_size, dtype=coupling.dtype)
    cumulative_decay = jnp.exp(log_prefix)
    keys_against_state = jnp.einsum(
        "dlu,lux->ldx", normalized_keys, initial_state, precision=PRECISION_MAXIMUM
    )
    right_side = write_rate.T[:, :, None] * (
        jnp.swapaxes(values, 0, 1) - cumulative_decay[:, :, None] * keys_against_state
    )
    value_updates = jax.scipy.linalg.solve_triangular(
        unit_lower, right_side, lower=True, unit_diagonal=True
    )
    query_keys = decay_ratio * jnp.einsum(
        "ihk,jhk->hij", normalized_queries, normalized_keys, precision=PRECISION_MAXIMUM
    )
    layer_outputs = cumulative_decay[:, :, None] * jnp.einsum(
        "dlu,lux->ldx", normalized_queries, initial_state, precision=PRECISION_MAXIMUM
    )
    layer_outputs = layer_outputs + jnp.einsum(
        "hij,hjv->hiv", query_keys, value_updates, precision=PRECISION_MAXIMUM
    )
    final_decay_weights = decay_ratio[:, -1, :]
    final_state = cumulative_decay[:, -1][:, None, None] * initial_state + jnp.einsum(
        "zg,gzi,zgq->ziq",
        final_decay_weights,
        normalized_keys,
        value_updates,
        precision=PRECISION_MAXIMUM,
    )
    return (jnp.swapaxes(layer_outputs, 0, 1), final_state)


def combine_maps(earlier, later):
    offset = later[0] + jnp.einsum(
        "hab,hbv->hav", later[1], earlier[0], precision=PRECISION_MAXIMUM
    )
    linear = jnp.einsum("hab,hbc->hac", later[1], earlier[1], precision=PRECISION_MAXIMUM)
    return (offset, linear)


def shards(
    queries,
    key_vectors,
    values,
    out_grad,
    hidden_in,
    decay_weight,
    write_weight,
    decay_bias,
    decay_log,
    write_bias,
    start_state,
):
    decay_logit = jnp.dot(hidden_in, decay_weight, preferred_element_type=jnp.float32)
    write_logit = jnp.dot(hidden_in, write_weight, preferred_element_type=jnp.float32)
    query_full = queries.astype(jnp.float32)
    key_full = key_vectors.astype(jnp.float32)
    value_full = values.astype(jnp.float32)
    initial_state = start_state[0]
    forward = partial(block_forward, decay_log, decay_bias, write_bias)
    primal, pullback = jax.vjp(
        forward, query_full, key_full, value_full, decay_logit, write_logit, initial_state
    )
    layer_outputs, final_state = primal
    local_grads = pullback((out_grad.astype(jnp.float32), jnp.zeros_like(final_state)))
    head_count = initial_state.shape[0]
    key_width = initial_state.shape[1]
    identity_block = jnp.broadcast_to(
        jnp.eye(key_width, dtype=jnp.float32), (head_count, key_width, key_width)
    )
    no_values = jnp.zeros(query_full.shape, jnp.float32)
    _, propagator = forward(
        query_full, key_full, no_values, decay_logit, write_logit, identity_block
    )
    transfer = jnp.swapaxes(propagator, 1, 2)
    summary = carried_in(
        (local_grads[5], transfer),
        SEQ,
        combine_maps,
        (jnp.zeros_like(initial_state), identity_block),
    )
    carry_grads = pullback((jnp.zeros_like(layer_outputs), summary[0]))
    totals = [local_grads[member] + carry_grads[member] for member in range(5)]
    decay_grads = totals[3].astype(jnp.bfloat16)
    write_grads = totals[4].astype(jnp.bfloat16)
    weight_terms = (
        jnp.einsum("td,th->dh", hidden_in, decay_grads, preferred_element_type=jnp.float32),
        jnp.einsum("td,th->dh", hidden_in, write_grads, preferred_element_type=jnp.float32),
    )
    grad_decay_weight, grad_write_weight = (
        over_copies(weight_terms[0].astype(jnp.bfloat16), SEQ).astype(jnp.float32),
        over_copies(weight_terms[1].astype(jnp.bfloat16), SEQ).astype(jnp.float32),
    )
    every_decay, every_write, decay_columns, write_columns = rows_first(
        (decay_grads, write_grads, decay_weight, write_weight), "head", (1, 1, 1, 1)
    )
    slice_width = hidden_in.shape[1] // lax.axis_size("head")
    first_row = lax.axis_index("head") * slice_width
    decay_rows = lax.dynamic_slice_in_dim(decay_columns, first_row, slice_width, 0)
    write_rows = lax.dynamic_slice_in_dim(write_columns, first_row, slice_width, 0)
    grad_hidden = jnp.einsum(
        "th,dh->td", every_decay, decay_rows, preferred_element_type=jnp.float32
    )
    grad_hidden = grad_hidden + jnp.einsum(
        "th,dh->td", every_write, write_rows, preferred_element_type=jnp.float32
    )
    return (
        totals[0].astype(jnp.bfloat16),
        totals[1].astype(jnp.bfloat16),
        totals[2].astype(jnp.bfloat16),
        grad_hidden.astype(jnp.bfloat16),
        grad_decay_weight,
        grad_write_weight,
    )


def solution(mesh):
    torus = Mesh(mesh.devices.reshape(4, 16, mesh.shape["head"]), ("seq_0", "seq_1", "head"))
    in_specs = (
        P(SEQ, "head", None),
        P(SEQ, "head", None),
        P(SEQ, "head", None),
        P(SEQ, "head", None),
        P(SEQ, None),
        P(None, "head"),
        P(None, "head"),
        P("head"),
        P("head"),
        P("head"),
        P(SEQ, "head", None, None),
    )
    out_specs = (
        P(SEQ, "head", None),
        P(SEQ, "head", None),
        P(SEQ, "head", None),
        P(SEQ, "head"),
        P(None, "head"),
        P(None, "head"),
    )
    return jax.shard_map(
        shards, mesh=torus, in_specs=in_specs, out_specs=out_specs, check_vma=False
    )
```

profile of v0, /device:TPU:6, one launch (start us, length us, event | category | flops | bytes accessed | tf_op | source)
XLA Modules:
  0.0 445.0 jit_solution(15250741205185053771)
XLA Ops:
  7.4 0.8 exponential_negate_fusion
  8.2 1.0 fusion.279
  9.6 1.1 copy.134
  11.6 1.0 fusion.23
  13.4 39.3 %custom-call.10 = f32[4,1,128,128]{2,3,1,0:T(8,128)S(1)} custom-call(f32[4,1,128,128]{3,2,1,0:T(8,128)S(1)} %get-tuple-element.59), custom_call_target="InvertDiagBlocksLowerTriangular" | custom-call | tf_op jit(solution)/shard_map/jvp(jit(_solve_triangular))/vmap()/triangular_solve/custom-call.1 | solution.py:98
  53.3 1.4 convolution_add_fusion.2
  55.8 0.7 copy-done.25
  56.4 0.8 fusion.59
  57.9 0.7 fusion.64
  59.0 0.7 fusion.35
  59.8 0.8 fusion.15
  60.6 1.5 fusion.49
  64.7 1.3 convolution_add_fusion.3
  66.3 71.0 %all-gather.12.cloned.1.call-done = f32[64,128,128]{2,1,0:T(8,128)} async-done(((f32[4,128,128]{2,1,0:T(8,128)}), f32[64,128,128]{2,1,0:T(8,128)}) %all-gather.12.cloned.1.call-update) | async-done | bytes 4194320 | tf_op jit(solution)/shard_map/all_gather | solution.py:27
  137.3 1.5 fusion.142
  138.8 0.7 copy-done.30
  139.5 1.3 fusion.314
  140.8 1.3 fusion.315
  142.2 1.3 fusion.316
  148.4 0.7 copy-done.22
  149.1 1.1 fusion.328
  150.5 63.3 %all-gather.10.cloned.1.call-done = f32[64,128,128]{2,1,0:T(8,128)} async-done(((f32[4,128,128]{2,1,0:T(8,128)}), f32[64,128,128]{2,1,0:T(8,128)}) %all-gather.10.cloned.1.call-update) | async-done | bytes 4194320 | tf_op jit(solution)/shard_map/all_gather | solution.py:27
  213.8 1.5 convolution_add_fusion.27
  215.3 2.3 convolution_add_fusion.26
  217.6 1.5 convolution_add_fusion.25
  219.2 1.4 convolution_add_fusion.24
  220.6 1.4 convolution_add_fusion.23
  222.1 1.4 convolution_add_fusion.22
  227.6 0.7 copy-done.46
  228.3 1.1 convolution_add_fusion.12
  229.5 0.8 multiply_reduce_fusion.5
  230.9 0.7 fusion.12
  231.6 3.4 fusion.88
  235.0 3.1 fusion.71
  238.1 4.8 %all-gather.16.cloned.1.call-done = f32[16,128,128]{2,1,0:T(8,128)} async-done(((f32[4,128,128]{2,1,0:T(8,128)}), f32[16,128,128]{2,1,0:T(8,128)}) %all-gather.16.cloned.1.call-update) | async-done | bytes 1048592 | tf_op jit(solution)/shard_map/all_gather | solution.py:27
  243.0 34.2 %all-gather.14.cloned.1.call-done = f32[16,128,128]{2,1,0:T(8,128)} async-done(((f32[4,128,128]{2,1,0:T(8,128)}), f32[16,128,128]{2,1,0:T(8,128)}) %all-gather.14.cloned.1.call-update) | async-done | bytes 1048592 | tf_op jit(solution)/shard_map/all_gather | solution.py:27
  277.2 1.4 convolution_add_fusion.11
  278.6 1.4 convolution_add_fusion.10
  280.0 1.4 convolution_add_fusion.9
  281.5 1.4 fusion.17
  283.4 1.4 fusion.39
  285.4 0.7 convolution_add_fusion
  286.1 10.9 %fusion.52 = f32[4,128,128]{2,1,0:T(8,128)} fusion(f32[4,128,128]{2,1,0:T(8,128)S(1)} %convolution_add_fusion, f32[4,1,128,128]{2,3,1,0:T(8,128)S(1)} %custom-call.10), kind=kOutput, calls=%fused_computation.117 | convolution fusion | flops 100663296 | bytes 786432 | tf_op jit(solution)/shard_map/transpose(jvp(jit(_solve_triangular)))/vmap()/triangular_solve/dot.0 | solution.py:98
  298.5 2.4 multiply_select_fusion
  301.3 1.1 reduce_window_sum.31
  302.6 1.1 reduce_window_sum.32
  304.1 1.5 broadcast_in_dim.140
  305.6 16.4 %all-to-all-start = ((bf16[64,2048,4]{1,2,0:T(4,128)(2,1)}), bf16[64,2048,4]{1,2,0:T(4,128)(2,1)}, u32[]{:S(2)}, u32[]{:S(2)}) async-start(bf16[64,2048,4]{1,2,0:T(4,128)(2,1)} %broadcast_in_dim.140), calls=%async_computation | async-start | bytes 2097152 | tf_op jit(solution)/shard_map/all_to_all | solution.py:39
  322.0 1.1 fusion.42
  323.1 0.8 copy.188
  324.6 48.9 %all-to-all-done = bf16[64,2048,4]{1,2,0:T(4,128)(2,1)} async-done(((bf16[64,2048,4]{1,2,0:T(4,128)(2,1)}), bf16[64,2048,4]{1,2,0:T(4,128)(2,1)}, u32[]{:S(2)}, u32[]{:S(2)}) %all-to-all-start) | async-done | bytes 1048608 | tf_op jit(solution)/shard_map/all_to_all | solution.py:39
  373.5 1.5 broadcast_in_dim.141
  375.1 7.6 %all-to-all-start.1 = ((bf16[64,2048,4]{1,2,0:T(4,128)(2,1)}), bf16[64,2048,4]{1,2,0:T(4,128)(2,1)}, u32[]{:S(2)}, u32[]{:S(2)}) async-start(bf16[64,2048,4]{1,2,0:T(4,128)(2,1)} %broadcast_in_dim.141), calls=%async_computation.1 | async-start | bytes 2097152 | tf_op jit(solution)/shard_map/all_to_all | solution.py:39
  382.7 0.8 fusion.13
  384.6 0.8 fusion.6
  386.0 0.8 fusion.2
  386.8 0.8 fusion.46
  387.8 0.8 copy.189
  388.6 0.8 copy.190
  389.4 13.2 %all-gather.4 = bf16[8,4,4352]{2,1,0:T(4,128)(2,1)S(1)} all-gather(bf16[1,4,4352]{2,1,0:T(4,128)(2,1)S(1)} %maximum_bitcast_fusion), channel_id=1, replica_groups=mesh['seq_0'=4,'seq_1'=16,'head'=8] {'head'}, dimensions={0}, use_global_device_ids=true | all-gather | bytes 313344 | tf_op jit(solution)/shard_map/all_gather | solution.py:52
  402.9 0.8 fusion.19
  403.8 2.3 convert_reduce_fusion.1
  406.1 29.9 %all-to-all-done.1 = bf16[64,2048,4]{1,2,0:T(4,128)(2,1)} async-done(((bf16[64,2048,4]{1,2,0:T(4,128)(2,1)}), bf16[64,2048,4]{1,2,0:T(4,128)(2,1)}, u32[]{:S(2)}, u32[]{:S(2)}) %all-to-all-start.1) | async-done | bytes 1048608 | tf_op jit(solution)/shard_map/all_to_all | solution.py:39
  436.0 2.3 convert_reduce_fusion
  (193 shorter events, 23.8 us)
Async XLA Ops:
  7.2 1.0 copy-start
  7.2 47.8 %copy-start.53 = (bf16[128,4,128]{2,1,0:T(4,128)(2,1)S(1)}, bf16[128,4,128]{2,1,0:T(4,128)(2,1)}, u32[]{:S(2)}) copy-start(bf16[128,4,128]{2,1,0:T(4,128)(2,1)} %param.15) | copy-start | bytes 393220
  7.2 47.9 %copy-start.3 = (f32[1,4,128,128]{3,2,1,0:T(8,128)S(1)}, f32[1,4,128,128]{3,2,1,0:T(8,128)}, u32[]{:S(2)}) copy-start(f32[1,4,128,128]{3,2,1,0:T(8,128)} %param.25) | copy-start | bytes 786436
  7.2 49.2 %copy-start.51 = (bf16[128,4,128]{2,1,0:T(4,128)(2,1)S(1)}, bf16[128,4,128]{2,1,0:T(4,128)(2,1)}, u32[]{:S(2)}) copy-start(bf16[128,4,128]{2,1,0:T(4,128)(2,1)} %param.17) | copy-start | bytes 393220
  7.2 130.1 %all-gather.12.cloned.1.call-start = ((), (), s32[]{:S(2)}) async-start(), calls=%async_computation.3 | async-start | bytes 4456448 | tf_op jit(solution)/shard_map/all_gather | solution.py:27
  7.4 51.3 %copy-start.47 = (bf16[128,4,128]{2,1,0:T(4,128)(2,1)S(1)}, bf16[128,4,128]{2,1,0:T(4,128)(2,1)}, u32[]{:S(2)}) copy-start(bf16[128,4,128]{2,1,0:T(4,128)(2,1)} %param.18) | copy-start | bytes 393220
  11.3 43.4 %copy-start.32 = (f32[4,128,128]{2,1,0:T(8,128)}, f32[4,128,128]{2,1,0:T(8,128)S(1)}, u32[]{:S(2)}) copy-start(f32[4,128,128]{2,1,0:T(8,128)S(1)} %fusion.28) | copy-start | bytes 786436
  54.7 159.1 %all-gather.10.cloned.1.call-start = ((), (), s32[]{:S(2)}) async-start(), calls=%async_computation.2 | async-start | bytes 4456448 | tf_op jit(solution)/shard_map/all_gather | solution.py:27
  55.7 0.7 copy-start.25
  59.0 81.8 %copy-start.7 = (f32[4,128,128]{2,1,0:T(8,128)}, f32[4,128,128]{2,1,0:T(8,128)S(1)}, u32[]{:S(2)}) copy-start(f32[4,128,128]{2,1,0:T(8,128)S(1)} %convolution_bitcast_fusion.8) | copy-start | bytes 786436
  60.6 2.1 copy-start.27
  64.3 73.0 %copy-start.23 = (f32[4,128,128]{2,1,0:T(8,128)}, f32[4,128,128]{2,1,0:T(8,128)S(1)}, u32[]{:S(2)}) copy-start(f32[4,128,128]{2,1,0:T(8,128)S(1)} %convolution_add_fusion.5) | copy-start | bytes 786436
  64.7 79.6 %copy-start.5 = (f32[4,128,128]{2,1,0:T(8,128)}, f32[4,128,128]{2,1,0:T(8,128)S(1)}, u32[]{:S(2)}) copy-start(f32[4,128,128]{2,1,0:T(8,128)S(1)} %fusion.57) | copy-start | bytes 786436
  66.0 177.0 %all-gather.16.cloned.1.call-start = ((), (), s32[]{:S(2)}) async-start(), calls=%async_computation.5 | async-start | bytes 1310720 | tf_op jit(solution)/shard_map/all_gather | solution.py:27
  137.3 6.2 %copy-start.1 = (f32[64,128,128]{2,1,0:T(8,128)S(1)}, f32[64,128,128]{2,1,0:T(8,128)}, u32[]{:S(2)}) copy-start(f32[64,128,128]{2,1,0:T(8,128)} %all-gather.12.cloned.1.call-done) | copy-start | bytes 12582916
  138.7 0.7 copy-start.30
  143.5 2.9 copy-start.10
  143.9 2.9 copy-start.12
  144.3 2.9 copy-start.13
  144.8 2.9 copy-start.14
  145.2 2.9 copy-start.15
  145.6 2.5 copy-start.16
  146.0 2.1 copy-start.17
  146.4 1.7 copy-start.18
  146.8 1.3 copy-start.19
  147.2 73.4 %copy-start.20 = (f32[4,128,128]{2,1,0:T(8,128)}, f32[4,128,128]{2,1,0:T(8,128)S(1)}, u32[]{:S(2)}) copy-start(f32[4,128,128]{2,1,0:T(8,128)S(1)} %fusion.325) | copy-start | bytes 786436
  147.7 0.7 copy-start.21
  148.4 0.7 copy-start.22
  150.2 127.0 %all-gather.14.cloned.1.call-start = ((), (), s32[]{:S(2)}) async-start(), calls=%async_computation.4 | async-start | bytes 1310720 | tf_op jit(solution)/shard_map/all_gather | solution.py:27
  213.8 5.3 %copy-start.2 = (f32[64,128,128]{2,1,0:T(8,128)S(1)}, f32[64,128,128]{2,1,0:T(8,128)}, u32[]{:S(2)}) copy-start(f32[64,128,128]{2,1,0:T(8,128)} %all-gather.12.cloned.1.call-done) | copy-start | bytes 12582916
  213.8 9.7 %copy-start.9 = (f32[64,128,128]{2,1,0:T(8,128)S(1)}, f32[64,128,128]{2,1,0:T(8,128)}, u32[]{:S(2)}) copy-start(f32[64,128,128]{2,1,0:T(8,128)} %all-gather.10.cloned.1.call-done) | copy-start | bytes 12582916
  215.3 8.6 %copy-start.31 = (f32[4,128,128]{2,1,0:T(8,128)}, f32[4,128,128]{2,1,0:T(8,128)S(1)}, u32[]{:S(2)}) copy-start(f32[4,128,128]{2,1,0:T(8,128)S(1)} %convolution_add_fusion.27) | copy-start | bytes 786436
  217.6 6.8 %copy-start.33 = (f32[4,128,128]{2,1,0:T(8,128)}, f32[4,128,128]{2,1,0:T(8,128)S(1)}, u32[]{:S(2)}) copy-start(f32[4,128,128]{2,1,0:T(8,128)S(1)} %convolution_add_fusion.26) | copy-start | bytes 786436
  219.2 5.7 %copy-start.34 = (f32[4,128,128]{2,1,0:T(8,128)}, f32[4,128,128]{2,1,0:T(8,128)S(1)}, u32[]{:S(2)}) copy-start(f32[4,128,128]{2,1,0:T(8,128)S(1)} %convolution_add_fusion.25) | copy-start | bytes 786436
  220.6 4.6 %copy-start.35 = (f32[4,128,128]{2,1,0:T(8,128)}, f32[4,128,128]{2,1,0:T(8,128)S(1)}, u32[]{:S(2)}) copy-start(f32[4,128,128]{2,1,0:T(8,128)S(1)} %convolution_add_fusion.24) | copy-start | bytes 786436
  222.1 3.6 copy-start.36
  223.5 1.7 copy-start.37
  224.0 2.5 copy-start.38
  224.4 2.5 copy-start.39
  224.8 2.1 copy-start.40
  225.2 2.1 copy-start.41
  225.7 1.7 copy-start.42
  225.7 4.6 %copy-start.24 = (f32[4,128,128]{2,1,0:T(8,128)S(1)}, f32[4,128,128]{2,1,0:T(8,128)}, u32[]{:S(2)}) copy-start(f32[4,128,128]{2,1,0:T(8,128)} %copy-done.23) | copy-start | bytes 786436
  226.1 1.3 copy-start.43
  226.5 0.9 copy-start.44
  226.9 0.7 copy-start.45
  227.6 0.7 copy-start.46
  228.3 6.7 %copy-start.11 = (f32[4,128,128]{2,1,0:T(8,128)S(1)}, f32[4,128,128]{2,1,0:T(8,128)}, u32[]{:S(2)}) copy-start(f32[4,128,128]{2,1,0:T(8,128)} %copy-done.10) | copy-start | bytes 786436
  243.0 38.5 %copy-start.4 = (f32[16,128,128]{2,1,0:T(8,128)S(1)}, f32[16,128,128]{2,1,0:T(8,128)}, u32[]{:S(2)}) copy-start(f32[16,128,128]{2,1,0:T(8,128)} %all-gather.16.cloned.1.call-done) | copy-start | bytes 3145732
  277.2 5.7 %copy-start.49 = (f32[4,128,128]{2,1,0:T(8,128)S(1)}, f32[4,128,128]{2,1,0:T(8,128)}, u32[]{:S(2)}) copy-start(f32[4,128,128]{2,1,0:T(8,128)} %fusion.88) | copy-start | bytes 786436
  277.2 5.7 %copy-start.50 = (f32[4,128,128]{2,1,0:T(8,128)S(1)}, f32[4,128,128]{2,1,0:T(8,128)}, u32[]{:S(2)}) copy-start(f32[4,128,128]{2,1,0:T(8,128)} %fusion.71) | copy-start | bytes 786436
  282.9 15.6 %copy-start.6 = (f32[4,128,128]{2,1,0:T(8,128)S(1)}, f32[4,128,128]{2,1,0:T(8,128)}, u32[]{:S(2)}) copy-start(f32[4,128,128]{2,1,0:T(8,128)} %copy-done.5) | copy-start | bytes 786436
  282.9 15.6 %copy-start.8 = (f32[4,128,128]{2,1,0:T(8,128)S(1)}, f32[4,128,128]{2,1,0:T(8,128)}, u32[]{:S(2)}) copy-start(f32[4,128,128]{2,1,0:T(8,128)} %copy-done.7) | copy-start | bytes 786436
  282.9 15.6 %copy-start.26 = (f32[4,128,128]{2,1,0:T(8,128)S(1)}, f32[4,128,128]{2,1,0:T(8,128)}, u32[]{:S(2)}) copy-start(f32[4,128,128]{2,1,0:T(8,128)} %copy-done.25) | copy-start | bytes 786436
  298.3 23.7 %copy-start.28 = (f32[128,4,128]{0,2,1:T(8,128)S(1)}, f32[128,4,128]{0,2,1:T(8,128)}, u32[]{:S(2)}) copy-start(f32[128,4,128]{0,2,1:T(8,128)} %copy-done.27) | copy-start | bytes 786436
  305.6 67.9 %all-to-all-start = ((bf16[64,2048,4]{1,2,0:T(4,128)(2,1)}), bf16[64,2048,4]{1,2,0:T(4,128)(2,1)}, u32[]{:S(2)}, u32[]{:S(2)}) async-start(bf16[64,2048,4]{1,2,0:T(4,128)(2,1)} %broadcast_in_dim.140), calls=%async_computation | async-start | bytes 2097152 | tf_op jit(solution)/shard_map/all_to_all | solution.py:39
  322.0 62.1 %copy-start.48 = (f32[4,128,128]{2,1,0:T(8,128)S(1)}, f32[4,128,128]{2,1,0:T(8,128)}, u32[]{:S(2)}) copy-start(f32[4,128,128]{2,1,0:T(8,128)} %get-tuple-element.78) | copy-start | bytes 786436
  322.0 62.6 %copy-start.29 = (f32[4,128,128]{2,1,0:T(8,128)S(1)}, f32[4,128,128]{2,1,0:T(8,128)}, u32[]{:S(2)}) copy-start(f32[4,128,128]{2,1,0:T(8,128)} %fusion.52) | copy-start | bytes 786436
  375.1 60.9 %all-to-all-start.1 = ((bf16[64,2048,4]{1,2,0:T(4,128)(2,1)}), bf16[64,2048,4]{1,2,0:T(4,128)(2,1)}, u32[]{:S(2)}, u32[]{:S(2)}) async-start(bf16[64,2048,4]{1,2,0:T(4,128)(2,1)} %broadcast_in_dim.141), calls=%async_computation.1 | async-start | bytes 2097152 | tf_op jit(solution)/shard_map/all_to_all | solution.py:39
  382.7 5.9 %copy-start.52 = (bf16[128,4,128]{2,0,1:T(8,128)(2,1)S(1)}, bf16[128,4,128]{2,0,1:T(8,128)(2,1)}, u32[]{:S(2)}) copy-start(bf16[128,4,128]{2,0,1:T(8,128)(2,1)} %get-tuple-element.62) | copy-start | bytes 393220
  382.7 6.7 %copy-start.54 = (bf16[2048,4]{0,1:T(4,128)(2,1)S(1)}, bf16[2048,4]{0,1:T(4,128)(2,1)}, u32[]{:S(2)}) copy-start(bf16[2048,4]{0,1:T(4,128)(2,1)} %param.20) | copy-start | bytes 49156
  382.7 6.7 %copy-start.55 = (bf16[2048,4]{0,1:T(4,128)(2,1)S(1)}, bf16[2048,4]{0,1:T(4,128)(2,1)}, u32[]{:S(2)}) copy-start(bf16[2048,4]{0,1:T(4,128)(2,1)} %param.21) | copy-start | bytes 49156
Sparse Core Ops, SparseCore 0:
  54.9 82.3 all-gather.11
  139.3 74.4 all-gather.9
  215.9 27.0 all-gather.15
  244.9 32.1 all-gather.13
where the time goes:
time: 445 us
  waiting for transfers between devices  252 us (57%)
  matrix products  76.8 us (17%)
  other arithmetic  51.5 us (12%)
  starting transfers between devices  24.8 us (6%)
  between operations  15.3 us (3%)
  blocking collectives  13.2 us (3%)
  local copies, waits for them, and re-layouts  11.1 us (2%)
    all_gather x4, waiting for transfers between devices, carried_in(): pieces = jax.tree.map(lambda part: lax.all_gather(part, axis), so_far)  173 us
    all_to_all x2, waiting for transfers between devices, sent_to_all(): lax.all_to_all(jnp.broadcast_to(array[None], (count, *array.shape)), axis...  78.8 us
    another operation x4, other arithmetic, block_forward(): jax.scipy.linalg.solve_triangular(unit_lower, right_side, lower=True, uni...  39.4 us
    all_to_all x2, starting transfers between devices, sent_to_all(): lax.all_to_all(jnp.broadcast_to(array[None], (count, *array.shape)), axis...  24 us
    dot_general x22, matrix products, combine_maps(): jnp.einsum('hab,hbv->hav', later[1], earlier[0], precision=PRECISION_MAXI...  23.8 us
    dot_general x17, matrix products, combine_maps(): jnp.einsum('hab,hbc->hac', later[1], earlier[1], precision=PRECISION_MAXI...  14 us
    another operation x6, matrix products, block_forward(): jax.scipy.linalg.solve_triangular(unit_lower, right_side, lower=True, uni...  14 us
    all_gather x1, blocking collectives, rows_first(): out, at, outs = (lax.all_gather(both, axis, axis=0, tiled=True), 0, [])  13.2 us
  transfers between devices with their start and end apart: 6, of which 6 were waited for; matrix products, arithmetic and copies ran while one was open for 13% of the time, Pallas kernels for 0%

commit v1 on v0

v1 whole, which is shorter than its diff:
```python
import functools

import jax
import jax.numpy as jnp
from jax import lax
from jax.experimental import pallas as pl
from jax.experimental.pallas import tpu as pltpu
from jax.sharding import Mesh
from jax.sharding import PartitionSpec as P

F32 = jnp.float32
BF16 = jnp.bfloat16
EPSILON = 1e-06
NN = (((1,), (0,)), ((), ()))
NT = (((1,), (1,)), ((), ()))
TN = (((0,), (0,)), ((), ()))
MESH = pl.DeviceIdType.MESH


def mm(a, b, dims=NN):
    return lax.dot_general(
        a.astype(BF16), b.astype(BF16), dims, preferred_element_type=F32
    )


def halves(a):
    high = a.astype(BF16)
    return high, (a - high.astype(F32)).astype(BF16)


def mm3(a, b, dims=NN):
    ah, al = halves(a)
    bh, bl = halves(b)
    return mm(ah, bh, dims) + (mm(ah, bl, dims) + mm(al, bh, dims))


def mm_ones(a, ones, dims=NN):
    high, rest = halves(a)
    mid = (a - high.astype(F32) - rest.astype(F32)).astype(BF16)
    return mm(high, ones, dims) + (mm(rest, ones, dims) + mm(mid, ones, dims))


def position_masks(n):
    row = lax.broadcasted_iota(jnp.int32, (n, n), 0)
    col = lax.broadcasted_iota(jnp.int32, (n, n), 1)
    return row, col


def gate_rows(logits, decay_bias, decay_scale, write_bias, heads):
    shifted = logits[:heads] + decay_bias
    soft = jnp.maximum(shifted, 0.0) + jnp.log1p(jnp.exp(-jnp.abs(shifted)))
    log_decay = -decay_scale * soft
    n = logits.shape[1]
    row, col = position_masks(n)
    upper = jnp.where(row <= col, 1.0, 0.0).astype(BF16)
    prefix = mm_ones(log_decay, upper)
    written = 1.0 / (1.0 + jnp.exp(-(logits[heads:] + write_bias)))
    slope = -decay_scale / (1.0 + jnp.exp(-shifted))
    return prefix, written, slope


def unit(x):
    scale = lax.rsqrt(jnp.sum(x * x, axis=-1, keepdims=True) + EPSILON)
    return x * scale, scale


def lockstep(fn, *lists):
    return [fn(*items) for items in zip(*lists)]


def first_half(qs, ks, vs, dys, states, prefix_rows, prefix_cols, write_cols):
    n = qs[0].shape[0]
    row, col = position_masks(n)
    lower, strict = row >= col, row > col
    qn = lockstep(unit, qs)
    kn = lockstep(unit, ks)
    q_scale = [s for _, s in qn]
    k_scale = [s for _, s in kn]
    qn = [x for x, _ in qn]
    kn = [x for x, _ in kn]
    ratio = lockstep(
        lambda c, r: jnp.where(lower, jnp.exp(jnp.where(lower, c - r, 0.0)), 0.0),
        prefix_cols,
        prefix_rows,
    )
    gram = lockstep(lambda k: mm3(k, k, NT), kn)
    gram = lockstep(lambda r, g: jnp.where(strict, r * g, 0.0), ratio, gram)
    coupling = lockstep(lambda b, g: b * g, write_cols, gram)
    near = (row ^ col) == 1
    inverse = lockstep(
        lambda c: jnp.where(row == col, 1.0, 0.0) - jnp.where(near, c, 0.0), coupling
    )
    size = 2
    while size < n:
        joint = ((row ^ col) >= size) & ((row ^ col) < 2 * size)
        part = lockstep(
            lambda c, t: mm3(jnp.where(joint, c, 0.0), t), coupling, inverse
        )
        inverse = lockstep(lambda t, p: t - mm3(t, p), inverse, part)
        size *= 2
    gain = lockstep(jnp.exp, prefix_cols)
    last = [c[n - 1 : n] for c in prefix_cols]
    tail = lockstep(lambda l, c: jnp.exp(l - c), last, prefix_cols)
    keyed = lockstep(lambda b, g, k: b * g * k, write_cols, gain, kn)
    solved = lockstep(mm, inverse, keyed)
    tailed = lockstep(lambda w, k: w * k, tail, kn)
    map_a = lockstep(lambda x, w: -mm(x, w, TN), solved, tailed)
    scores = lockstep(lambda q, k, r: r * mm(q, k, NT), qn, kn, ratio)
    reach = lockstep(lambda g, q, p, x: g * q - mm(p, x), gain, qn, scores, solved)
    map_b = lockstep(lambda r, d: mm(r, d, TN), reach, dys)
    return dict(
        qn=qn, kn=kn, q_scale=q_scale, k_scale=k_scale, ratio=ratio, gram=gram,
        coupling=coupling, inverse=inverse, gain=gain, tail=tail, tailed=tailed,
        scores=scores, map_a=map_a, map_b=map_b,
    )


def between(vs, dys, states, write_cols, f):
    n = vs[0].shape[0]
    row, col = position_masks(n)
    lower = row >= col
    key_state = lockstep(mm, f["kn"], states)
    error = lockstep(lambda v, g, s: v - g * s, vs, f["gain"], key_state)
    updates = lockstep(lambda t, b, e: mm(t, b * e), f["inverse"], write_cols, error)
    pulled = lockstep(lambda p, d: mm(p, d, TN), f["scores"], dys)
    d_scores = lockstep(lambda d, u: jnp.where(lower, mm(d, u, NT), 0.0), dys, updates)
    d_qk = lockstep(lambda r, d: r * d, f["ratio"], d_scores)
    out_state = lockstep(lambda g, d, s: g * mm(d, s, NT), f["gain"], dys, states)
    d_qn = lockstep(lambda o, d, k: o + mm(d, k), out_state, d_qk, f["kn"])
    d_q = lockstep(
        lambda d, q, s: s * (d - q * jnp.sum(q * d, axis=-1, keepdims=True)),
        d_qn, f["qn"], f["q_scale"],
    )
    d_kn = lockstep(lambda d, q: mm(d, q, TN), d_qk, f["qn"])
    paired = lockstep(lambda d, p: d * p, d_scores, f["scores"])
    gain_q = lockstep(
        lambda o, q: jnp.sum(o * q, axis=-1, keepdims=True), out_state, f["qn"]
    )
    return dict(
        key_state=key_state, error=error, updates=updates, pulled=pulled, d_q=d_q,
        d_kn=d_kn, paired=paired, gain_q=gain_q,
    )


def second_half(states, write_cols, f, g, ends):
    n = states[0].shape[0]
    row, col = position_masks(n)
    strict = row > col
    d_updates = lockstep(lambda p, w, d: p + mm(w, d), g["pulled"], f["tailed"], ends)
    d_right = lockstep(lambda t, d: mm(t, d, TN), f["inverse"], d_updates)
    d_v = lockstep(lambda b, d: b * d, write_cols, d_right)
    d_couple = lockstep(
        lambda d, u: jnp.where(strict, -mm(d, u, NT), 0.0), d_right, g["updates"]
    )
    d_gram = lockstep(lambda b, r, d: b * r * d, write_cols, f["ratio"], d_couple)
    right_state = lockstep(
        lambda b, c, d, s: b * c * mm(d, s, NT), write_cols, f["gain"], d_right, states
    )
    tail_keys = lockstep(lambda w, u, d: w * mm(u, d, NT), f["tail"], g["updates"], ends)
    d_kn = lockstep(
        lambda a, r, t, m, k: a - r + t + (mm(m, k) + mm(m, k, TN)),
        g["d_kn"], right_state, tail_keys, d_gram, f["kn"],
    )
    d_k = lockstep(
        lambda d, k, s: s * (d - k * jnp.sum(k * d, axis=-1, keepdims=True)),
        d_kn, f["kn"], f["k_scale"],
    )
    d_write = lockstep(
        lambda d, e, m, c: jnp.sum(d * e + m * c, axis=-1, keepdims=True),
        d_right, g["error"], d_couple, f["gram"],
    )
    pairs = lockstep(lambda m, c, p: m * c + p, d_couple, f["coupling"], g["paired"])
    tail_sum = lockstep(
        lambda k, t: jnp.sum(k * t, axis=-1, keepdims=True), f["kn"], tail_keys
    )
    at_end = lax.broadcasted_iota(jnp.int32, (n, 1), 0) == n - 1
    d_prefix = lockstep(
        lambda p, q, b, c, d, s, t, st, e: jnp.sum(p, axis=-1, keepdims=True)
        + q
        - b * c * jnp.sum(d * s, axis=-1, keepdims=True)
        - t
        + jnp.where(
            at_end,
            jnp.sum(t, axis=0, keepdims=True)
            + c[n - 1 : n]
            * jnp.sum(jnp.sum(st * e, axis=-1, keepdims=True), axis=0, keepdims=True),
            0.0,
        ),
        pairs, g["gain_q"], write_cols, f["gain"], d_right, g["key_state"], tail_sum,
        states, ends,
    )
    d_prefix_row = lockstep(lambda p: jnp.sum(p, axis=0, keepdims=True), pairs)
    return d_v, d_k, d_write, d_prefix, d_prefix_row


def gate_grads(d_prefix, d_write, written, slope):
    n = d_prefix.shape[1]
    row, col = position_masks(n)
    later = jnp.where(row >= col, 1.0, 0.0).astype(BF16)
    d_decay_logit = mm_ones(d_prefix, later) * slope
    d_write_logit = d_write * written * (1.0 - written)
    return jnp.concatenate([d_decay_logit, d_write_logit], axis=0)


def join(map_a, map_b, own_decay, in_a, in_b, in_decay):
    wide = mm(map_a, jnp.concatenate([in_a, in_b], axis=1))
    n = in_a.shape[1]
    new_a = wide[:, :n] + own_decay * in_a.astype(F32) + in_decay * map_a.astype(F32)
    new_b = wide[:, n:] + own_decay * in_b.astype(F32) + map_b.astype(F32)
    return new_a, new_b


def applied(map_a, map_b, decay, x):
    return map_b.astype(F32) + decay * x.astype(F32) + mm(map_a, x)


def kernel(
    sizes, axes,
    q_ref, k_ref, v_ref, dy_ref, hid_ref, wd_ref, ww_ref, s0_ref,
    dbias_ref, dlog_ref, wbias_ref,
    gq_ref, gk_ref, gv_ref, gh_ref, gdw_ref, gww_ref,
    qs, ks, vs, ds, wt, wall, gall, glr, own_a, own_b,
    m1r, m1s, m2r, m2s, fr, fs, gr, pw, rsr, xs, xr, wf,
    w_sem, g_sem, gl_sem, m1_sem, m2_sem, f_sem, gr_sem, rs_sem, x_sem, wf_sem,
    w_out, g_out, gl_out, m1_out, m2_out, f_out, d_out, gr_out, rs_out, x_out, wf_out,
):
    nx, na, nb, nh = sizes
    nz = na * nb
    heads, n = s0_ref.shape[0], s0_ref.shape[1]
    rows = 2 * heads
    width = hid_ref.shape[1] // nh
    piece = hid_ref.shape[1] // nz
    x, z, h = (lax.axis_index(axis) for axis in axes)
    a, b = z // nb, z % nb
    every = list(range(heads))

    def put(src, dst, send, recv, at):
        return pltpu.make_async_remote_copy(
            src_ref=src, dst_ref=dst, send_sem=send, recv_sem=recv,
            device_id=at, device_id_type=MESH,
        )

    def z_peer(i):
        return lax.rem(z + i, nz)

    def x_peer(i):
        return lax.rem(x + i, nx)

    def h_peer(i):
        return lax.rem(h + i, nh)

    barrier = pltpu.get_barrier_semaphore()
    for i in range(1, nz):
        pl.semaphore_signal(
            barrier, inc=1, device_id=(x, z_peer(i), h), device_id_type=MESH
        )
    for i in range(1, nx):
        pl.semaphore_signal(
            barrier, inc=1, device_id=(x_peer(i), z, h), device_id_type=MESH
        )
    for i in range(1, nh):
        pl.semaphore_signal(
            barrier, inc=1, device_id=(x, z, h_peer(i)), device_id_type=MESH
        )

    qs[...] = q_ref[...].astype(F32)
    ks[...] = k_ref[...].astype(F32)
    vs[...] = v_ref[...].astype(F32)
    ds[...] = dy_ref[...].astype(F32)

    def head_rows(ref):
        return [ref[pl.ds(i, n, stride=heads), :] for i in every]

    q, k, v, dy = head_rows(qs), head_rows(ks), head_rows(vs), head_rows(ds)
    states = [s0_ref[i] for i in every]
    wt[...] = jnp.concatenate(
        [wd_ref[...].astype(F32), ww_ref[...].astype(F32)], axis=0
    ).astype(BF16)
    logits = mm(wt[...], hid_ref[...], NT)
    where = lax.broadcasted_iota(jnp.int32, (heads, n), 0)

    def spread(ref):
        out = jnp.full((heads, n), ref[0], F32)
        for i in every[1:]:
            out = jnp.where(where == i, ref[i], out)
        return out

    prefix, written, slope = gate_rows(
        logits, spread(dbias_ref), jnp.exp(spread(dlog_ref)), spread(wbias_ref), heads
    )
    both = jnp.concatenate([prefix, written], axis=0)
    glr[z] = both
    turned = both.T
    prefix_cols = [turned[:, i : i + 1] for i in every]
    write_cols = [turned[:, heads + i : heads + i + 1] for i in every]
    prefix_rows = [prefix[i : i + 1] for i in every]

    pl.semaphore_wait(barrier, (nz - 1) + (nx - 1) + (nh - 1))

    sent = []
    for i in range(1, nz):
        copy = put(
            glr.at[z], glr.at[z], gl_out.at[i], gl_sem.at[z], (x, z_peer(i), h)
        )
        copy.start()
        sent.append(copy)
    for i in range(1, nh):
        to = h_peer(i)
        copy = put(
            wt.at[:, pl.ds(pl.multiple_of(to * width, 128), width)],
            wall.at[h], w_out.at[i], w_sem.at[h], (x, z, to),
        )
        copy.start()
        sent.append(copy)
    wall[h] = wt[:, pl.ds(pl.multiple_of(h * width, 128), width)]

    f = first_half(q, k, v, dy, states, prefix_rows, prefix_cols, write_cols)
    for i in every:
        own_a[i] = f["map_a"][i]
        own_b[i] = f["map_b"][i]

    @pl.when(b == nb - 1)
    def _():
        m1r[...] = jnp.zeros_like(m1r)

    @pl.when(a == na - 1)
    def _():
        m2r[...] = jnp.zeros_like(m2r)

    @pl.when(x == nx - 1)
    def _():
        fr[...] = jnp.zeros_like(fr)

    for i in range(1, nz):
        put(
            glr.at[z], glr.at[z_peer(i)], gl_out.at[i], gl_sem.at[z_peer(i)], (x, z, h)
        ).wait_recv()

    in_group = jnp.zeros((rows, n), F32)
    in_line = jnp.zeros((rows, n), F32)
    for i in range(nz):
        tile = glr[i]
        in_group = in_group + jnp.where((i > z) & (i < (a + 1) * nb), tile, 0.0)
        in_line = in_line + jnp.where(i >= (a + 1) * nb, tile, 0.0)
    own_decay = jnp.exp(both)
    group_decay = jnp.exp(in_group)
    line_decay = jnp.exp(in_line)
    whole_decay = jnp.exp(both + in_group)
    full_decay = jnp.exp(both + in_group + in_line)

    def scalar(tile, i):
        return tile[i : i + 1, n - 1 : n]

    for i in every:
        @pl.when(b < nb - 1)
        def _():
            put(
                m1s.at[i], m1r.at[i], m1_out.at[i], m1_sem.at[i], (x, z, h)
            ).wait_recv()

        new_a, new_b = join(
            own_a[i], own_b[i], scalar(own_decay, i),
            m1r[i, 0], m1r[i, 1], scalar(group_decay, i),
        )
        m1s[i, 0] = new_a.astype(BF16)
        m1s[i, 1] = new_b.astype(BF16)

        @pl.when(b > 0)
        def _():
            put(
                m1s.at[i], m1r.at[i], m1_out.at[i], m1_sem.at[i], (x, z - 1, h)
            ).start()

        @pl.when(b == 0)
        def _():
            @pl.when(a < na - 1)
            def _():
                put(
                    m2s.at[i], m2r.at[i], m2_out.at[i], m2_sem.at[i], (x, z, h)
                ).wait_recv()

            line_a, line_b = join(
                m1s[i, 0], m1s[i, 1], scalar(whole_decay, i),
                m2r[i, 0], m2r[i, 1], scalar(line_decay, i),
            )
            m2s[i, 0] = line_a.astype(BF16)
            m2s[i, 1] = line_b.astype(BF16)

            @pl.when(a > 0)
            def _():
                put(
                    m2s.at[i], m2r.at[i], m2_out.at[i], m2_sem.at[i], (x, z - nb, h)
                ).start()

    @pl.when(b == 0)
    def _():
        for i in every:
            @pl.when((a > 0) | (x < nx - 1))
            def _():
                put(fs.at[i], fr.at[i], f_out.at[i], f_sem.at[i], (x, z, h)).wait_recv()

            @pl.when(a == 0)
            def _():
                @pl.when(x > 0)
                def _():
                    fs[i] = applied(
                        m2s[i, 0], m2s[i, 1], scalar(full_decay, i), fr[i]
                    ).astype(BF16)
                    put(
                        fs.at[i], fr.at[i], f_out.at[i], f_sem.at[i], (x - 1, z, h)
                    ).start()

                for j in range(1, na):
                    put(
                        fr.at[i], fr.at[i], d_out.at[i, j], f_sem.at[i], (x, j * nb, h)
                    ).start()

            gr[i] = applied(
                m2r[i, 0], m2r[i, 1], scalar(line_decay, i), fr[i]
            ).astype(BF16)
            for j in range(1, nb):
                put(
                    gr.at[i], gr.at[i], gr_out.at[i, j], gr_sem.at[i], (x, z + j, h)
                ).start()

    g = between(v, dy, states, write_cols, f)
    for i in every:
        gq_scratch = g["d_q"][i]
        qs[pl.ds(i, n, stride=heads), :] = gq_scratch
    gq_ref[...] = qs[...].astype(BF16)

    @pl.when(b > 0)
    def _():
        for i in every:
            put(gr.at[i], gr.at[i], gr_out.at[i, 1], gr_sem.at[i], (x, z, h)).wait_recv()

    ends = [
        applied(m1r[i, 0], m1r[i, 1], scalar(group_decay, i), gr[i]) for i in every
    ]
    d_v, d_k, d_write, d_prefix, d_prefix_row = second_half(
        states, write_cols, f, g, ends
    )
    columns = jnp.concatenate(d_prefix + d_write, axis=1).T
    grads = gate_grads(
        columns[:heads] - jnp.concatenate(d_prefix_row, axis=0),
        columns[heads:], written, slope,
    ).astype(BF16)
    gall[h] = grads
    for i in range(1, nh):
        copy = put(
            gall.at[h], gall.at[h], g_out.at[i], g_sem.at[h], (x, z, h_peer(i))
        )
        copy.start()
        sent.append(copy)
    for j in range(nz):
        pw[j] = mm(grads, hid_ref[:, j * piece : (j + 1) * piece]).astype(BF16)
    for i in range(1, nz):
        to = z_peer(i)
        copy = put(pw.at[to], rsr.at[z], rs_out.at[i], rs_sem.at[z], (x, to, h))
        copy.start()
        sent.append(copy)
    rsr[z] = pw[z]

    for i in every:
        ks[pl.ds(i, n, stride=heads), :] = d_k[i]
        vs[pl.ds(i, n, stride=heads), :] = d_v[i]
    gk_ref[...] = ks[...].astype(BF16)
    gv_ref[...] = vs[...].astype(BF16)

    for i in range(1, nh):
        put(
            wall.at[h], wall.at[h_peer(i)], w_out.at[i], w_sem.at[h_peer(i)], (x, z, h)
        ).wait_recv()
        put(
            gall.at[h], gall.at[h_peer(i)], g_out.at[i], g_sem.at[h_peer(i)], (x, z, h)
        ).wait_recv()
    total = jnp.zeros((n, width), F32)
    for i in range(nh):
        total = total + mm(gall[i], wall[i], TN)
    gh_ref[...] = total.astype(BF16)

    for i in range(1, nz):
        put(
            pw.at[0], rsr.at[z_peer(i)], rs_out.at[i], rs_sem.at[z_peer(i)], (x, z, h)
        ).wait_recv()
    acc = rsr[0].astype(F32)
    for i in range(1, nz):
        acc = acc + rsr[i].astype(F32)
    xs[...] = acc.astype(BF16)
    for i in range(1, nx):
        copy = put(xs, xr.at[x], x_out.at[i], x_sem.at[x], (x_peer(i), z, h))
        copy.start()
        sent.append(copy)
    xr[x] = xs[...]
    for i in range(1, nx):
        put(
            xs, xr.at[x_peer(i)], x_out.at[i], x_sem.at[x_peer(i)], (x, z, h)
        ).wait_recv()
    acc = xr[0].astype(F32)
    for i in range(1, nx):
        acc = acc + xr[i].astype(F32)
    wf[z] = acc.astype(BF16)
    for i in range(1, nz):
        copy = put(
            wf.at[z], wf.at[z], wf_out.at[i], wf_sem.at[z], (x, z_peer(i), h)
        )
        copy.start()
        sent.append(copy)
    for i in range(1, nz):
        put(
            wf.at[z], wf.at[z_peer(i)], wf_out.at[i], wf_sem.at[z_peer(i)], (x, z, h)
        ).wait_recv()
    for j in range(nz):
        tile = wf[j].astype(F32)
        gdw_ref[:, j * piece : (j + 1) * piece] = tile[:heads]
        gww_ref[:, j * piece : (j + 1) * piece] = tile[heads:]

    for copy in sent:
        copy.wait_send()

    @pl.when(b > 0)
    def _():
        for i in every:
            put(m1s.at[i], m1r.at[i], m1_out.at[i], m1_sem.at[i], (x, z, h)).wait_send()

    @pl.when(b == 0)
    def _():
        @pl.when(a > 0)
        def _():
            for i in every:
                put(
                    m2s.at[i], m2r.at[i], m2_out.at[i], m2_sem.at[i], (x, z, h)
                ).wait_send()

        @pl.when(a == 0)
        def _():
            @pl.when(x > 0)
            def _():
                for i in every:
                    put(fs.at[i], fr.at[i], f_out.at[i], f_sem.at[i], (x, z, h)).wait_send()

            for i in every:
                for j in range(1, na):
                    put(
                        fr.at[i], fr.at[i], d_out.at[i, j], f_sem.at[i], (x, z, h)
                    ).wait_send()

        for i in every:
            for j in range(1, nb):
                put(
                    gr.at[i], gr.at[i], gr_out.at[i, j], gr_sem.at[i], (x, z, h)
                ).wait_send()


def shards(sizes, axes, q, k, v, dy, hid, wd, ww, dbias, dlog, wbias, s0):
    nx, na, nb, nh = sizes
    nz = na * nb
    n, heads, dk = q.shape
    depth = hid.shape[1]
    rows, flat = 2 * heads, (n * heads, dk)
    width, piece = depth // nh, depth // nz
    vmem = pl.BlockSpec(memory_space=pltpu.VMEM)
    smem = pl.BlockSpec(memory_space=pltpu.SMEM)
    dma = pltpu.SemaphoreType.DMA
    maps = pltpu.VMEM((heads, 2, dk, dk), BF16)
    ends = pltpu.VMEM((heads, dk, dk), BF16)
    out = pl.pallas_call(
        functools.partial(kernel, sizes, axes),
        out_shape=(
            jax.ShapeDtypeStruct(flat, BF16),
            jax.ShapeDtypeStruct(flat, BF16),
            jax.ShapeDtypeStruct(flat, BF16),
            jax.ShapeDtypeStruct((n, width), BF16),
            jax.ShapeDtypeStruct((heads, depth), F32),
            jax.ShapeDtypeStruct((heads, depth), F32),
        ),
        in_specs=[vmem] * 8 + [smem] * 3,
        out_specs=[vmem] * 6,
        scratch_shapes=[
            pltpu.VMEM(flat, F32), pltpu.VMEM(flat, F32),
            pltpu.VMEM(flat, F32), pltpu.VMEM(flat, F32),
            pltpu.VMEM((rows, depth), BF16),
            pltpu.VMEM((nh, rows, width), BF16),
            pltpu.VMEM((nh, rows, n), BF16),
            pltpu.VMEM((nz, rows, n), F32),
            pltpu.VMEM((heads, dk, dk), F32), pltpu.VMEM((heads, dk, dk), F32),
            maps, maps, maps, maps, ends, ends, ends,
            pltpu.VMEM((nz, rows, piece), BF16), pltpu.VMEM((nz, rows, piece), BF16),
            pltpu.VMEM((rows, piece), BF16), pltpu.VMEM((nx, rows, piece), BF16),
            pltpu.VMEM((nz, rows, piece), BF16),
            dma((nh,)), dma((nh,)), dma((nz,)), dma((heads,)), dma((heads,)),
            dma((heads,)), dma((heads,)), dma((nz,)), dma((nx,)), dma((nz,)),
            dma((nh,)), dma((nh,)), dma((nz,)), dma((heads,)), dma((heads,)),
            dma((heads,)), dma((heads, na)), dma((heads, nb)),
            dma((nz,)), dma((nx,)), dma((nz,)),
        ],
        compiler_params=pltpu.CompilerParams(
            collective_id=0, has_side_effects=True, vmem_limit_bytes=48 * 2**20
        ),
    )(
        q.reshape(flat), k.reshape(flat), v.reshape(flat), dy.reshape(flat),
        hid, wd.T, ww.T, s0[0], dbias, dlog, wbias,
    )
    gq, gk, gv, gh, gdw, gww = out
    return (
        gq.reshape(q.shape), gk.reshape(q.shape), gv.reshape(q.shape),
        gh, gdw.T, gww.T,
    )


def solution(mesh):
    return build(mesh, (4, 4, 4))


def build(mesh, split):
    nx, na, nb = split
    nh = mesh.shape["head"]
    torus = Mesh(mesh.devices.reshape(nx, na * nb, nh), ("x", "z", "head"))
    seq = ("x", "z")
    by_head = P(seq, "head", None)
    in_specs = (
        by_head, by_head, by_head, by_head, P(seq, None),
        P(None, "head"), P(None, "head"), P("head"), P("head"), P("head"),
        P(seq, "head", None, None),
    )
    out_specs = (
        by_head, by_head, by_head, P(seq, "head"), P(None, "head"), P(None, "head"),
    )
    return jax.shard_map(
        functools.partial(shards, (nx, na, nb, nh), ("x", "z", "head")),
        mesh=torus, in_specs=in_specs, out_specs=out_specs, check_vma=False,
    )
```

time: 445 us -> 113 us (0.25)
  waiting for transfers between devices: 252 us -> 0 us
  Pallas kernels: 0 us -> 100 us
  matrix products: 76.8 us -> 0 us
  other arithmetic: 51.5 us -> 0 us
  starting transfers between devices: 24.8 us -> 0 us
  between operations: 15.3 us -> 0.68 us
  blocking collectives: 13.2 us -> 0 us
    all_gather x4 -> x0, waiting for transfers between devices: 173 us -> none  [carried_in(): pieces = jax.tree.map(lambda part: lax.all_gather(part, axis), so_far)]
    pallas_call x0 -> x1, Pallas kernels: none -> 100 us  [shards(): pl.pallas_call(functools.partial(kernel, sizes, axes), out_shape=(jax.Sha...]
    all_to_all x2 -> x0, waiting for transfers between devices: 78.8 us -> none  [sent_to_all(): lax.all_to_all(jnp.broadcast_to(array[None], (count, *array.shape)), axis...]
    dot_general x74 -> x0, matrix products: 62.8 us -> none  [the longest x22 23.8 us: combine_maps(): jnp.einsum('hab,hbv->hav', later[1], earlier[0], precision=PRECISION_MAXI...]
    another operation x7 -> x0, other arithmetic: 41.8 us -> none  [the longest x4 39.4 us: block_forward(): jax.scipy.linalg.solve_triangular(unit_lower, right_side, lower=True, uni...]
    all_to_all x2 -> x0, starting transfers between devices: 24 us -> none  [sent_to_all(): lax.all_to_all(jnp.broadcast_to(array[None], (count, *array.shape)), axis...]
    another operation x6 -> x0, matrix products: 14 us -> none  [block_forward(): jax.scipy.linalg.solve_triangular(unit_lower, right_side, lower=True, uni...]
    all_gather x1 -> x0, blocking collectives: 13.2 us -> none  [rows_first(): out, at, outs = (lax.all_gather(both, axis, axis=0, tiled=True), 0, [])]
  transfers between devices with their start and end apart: 6 -> 0, of which waited for: 6 -> 0; matrix products, arithmetic and copies ran while one was open for 13% -> 0% of each run, Pallas kernels for 0% -> 0%
where the time goes in v1:
time: 113 us; the launch traced here: 112 us
  Pallas kernels  100 us (88%)
  local copies, waits for them, and re-layouts  11.5 us (10%)
    pallas_call x1, Pallas kernels, shards(): pl.pallas_call(functools.partial(kernel, sizes, axes), out_shape=(jax.Sha...  100 us
    unnamed x28, local copies, waits for them, and re-layouts  11.5 us

profile of v1, /device:TPU:6, one launch (start us, length us, event | category | flops | bytes accessed | tf_op | source)
XLA Modules:
  0.0 112.4 jit_solution(3788815943603091215)
XLA Ops:
  0.6 0.0 copy-start.8
  0.6 0.0 copy-start.9
  0.7 0.0 copy-start.10
  0.7 0.6 copy-done.8
  1.3 0.0 copy-done.9
  1.3 0.0 copy-done.10
  1.3 0.0 copy-start
  1.3 1.0 copy-done
  2.4 0.0 copy-start.1
  2.4 0.9 copy-done.1
  3.3 0.0 copy-start.2
  3.3 0.9 copy-done.2
  4.2 0.0 copy-start.3
  4.2 0.9 copy-done.3
  5.1 0.0 copy-start.4
  5.1 0.9 copy-done.4
  6.0 0.0 copy-start.5
  6.0 0.9 copy-done.5
  6.9 0.0 copy-start.6
  6.9 0.7 copy-done.6
  7.7 0.0 copy-start.7
  7.7 0.7 copy-done.7
  8.4 100.2 %shard_map.154 = (bf16[512,128]{1,0:T(8,128)(2,1)S(1)}, bf16[512,128]{1,0:T(8,128)(2,1)S(1)}, bf16[512,128]{1,0:T(8,128)(2,1)S(1)}, bf16[128,256]{1,0:T(8,128)(2...) custom-call(bf16[512,128]{1,0:T(8,128)(2,1)S(1)} %bitcast.16, bf16[512,128]{1,0:T(8,128)(2,1)S(1)} %bitcast.17, ...), custom_call_target="tpu_custom_call" | custom-call | tf_op jit(solution)/shard_map/pallas_call | solution.py:567
  108.5 0.7 copy.23
  109.2 0.7 copy.24
  109.9 0.7 copy.25
  110.5 0.6 copy.26
  111.1 0.6 copy.27
  111.8 0.6 copy.28
Async XLA Ops:
  0.6 0.7 copy-start.8
  0.6 0.7 copy-start.9
  0.7 0.7 copy-start.10
  1.3 1.0 copy-start
  2.4 0.9 copy-start.1
  3.3 0.9 copy-start.2
  4.2 0.9 copy-start.3
  5.1 0.9 copy-start.4
  6.0 0.9 copy-start.5
  6.9 0.7 copy-start.6
  7.7 0.7 copy-start.7
